TPU v7x, 256 devices: a whole 4x4x8 slice. The times are simulated.
256 devices in a mesh: dp: 32 (over x, z_lo, core), sub: 8 (over z_hi, y).
Axes of the slice: x: 4, y: 4, z: 8 (z_hi: 2, z_lo: 4; z = z_hi * 4 + z_lo), core: 2. Of those that a mesh axis runs over, the one named last changes fastest.
Arguments:
- context: bfloat16 [403456, 1024], P(('dp', 'sub')), may hold values from -6 to 6
- target: bfloat16 [403456, 1024], P(('dp', 'sub')), may hold values from -16 to 16
- weight: float32 [1024, 1024], P(('dp', 'sub')), may hold values from -0.1875 to 0.1875
- stale: bfloat16 [256, 1024, 1024], P(('dp', 'sub')), may hold values from -1.25 to 1.25
- trigger: int32 [256, 16], P(('dp', 'sub')), may hold values 0 or 1
- aggregate: float32 [1024, 1024], P(('dp', 'sub')), may hold values from -3 to 3
- moment: float32 [1024, 1024], P(('dp', 'sub')), may hold values from -0.6 to 0.6
- second: float32 [1024, 1024], P(('dp', 'sub')), may hold values from 0.0001 to 0.01
Outputs:
- aggregate_new: float32 [1024, 1024], P(('dp', 'sub'))
- weight_new: float32 [1024, 1024], P(('dp', 'sub'))
- moment_new: float32 [1024, 1024], P(('dp', 'sub'))
- second_new: float32 [1024, 1024], P(('dp', 'sub'))
- stale_new: bfloat16 [256, 1024, 1024], P(('dp', 'sub'))
- norms: float32 [16], replicated
All inputs are finite; a program needn't handle non-finite values. No bound on the sum of `trigger` on one device may be relied on, other than what follows from the above.
Results may differ from a plain program's by a relative error of at most 0.006.
Values may be sent and summed in bfloat16 or wider, within the bound.
A program may use at most 64 MiB of HBM per device.

v0:
```python
import functools
import jax
import jax.numpy as jnp
from jax import lax
from jax.sharding import Mesh
from jax.sharding import PartitionSpec as P

SUB = ("sub_0", "sub_1")
DP = ("dp_0", "dp_1", "dp_2")
DP_SUB = ("dp_0", "dp_1", "dp_2", "sub_0", "sub_1")


def laid_out(pieces, dim):
    lengths = list(pieces.shape[1:])
    lengths[dim] *= pieces.shape[0]
    return jnp.moveaxis(pieces, 0, dim).reshape(lengths)


def sent_to_all(value, axis):
    copies = jnp.broadcast_to(value, (lax.axis_size(axis), *value.shape))
    return lax.all_to_all(copies, axis, split_axis=0, concat_axis=0, tiled=True)


def gathered_copies(value, axis, dim):
    return laid_out(sent_to_all(value, axis), dim)


def one_axis_at_a_time(value, axes):
    return functools.reduce(lax.psum, axes, value)


def in_blocks(value, dim, devices):
    lengths = value.shape
    pieces = value.reshape(*lengths[:dim], devices, lengths[dim] // devices, *lengths[dim + 1 :])
    return jnp.moveaxis(pieces, dim, 0)


def sent_and_summed(value, axis, dim):
    pieces = in_blocks(value, dim, lax.axis_size(axis))
    arrived = lax.all_to_all(pieces, axis, split_axis=0, concat_axis=0, tiled=True)
    return arrived.astype(jnp.float32).sum(axis=0)


def body(context, target, weight, stale, trigger, aggregate, moment, second):
    rows = context.shape[0]
    width = context.shape[1]
    owned = weight.shape[0]
    blocks = trigger.shape[1]
    span = width // blocks
    low_rows = weight.astype(jnp.bfloat16)
    low_group = gathered_copies(low_rows, SUB, 0)
    low_whole = lax.all_gather(low_group, DP, axis=0, tiled=True)
    output = jnp.dot(context, low_whole, preferred_element_type=jnp.float32)
    error = (output - target.astype(jnp.float32)).astype(jnp.bfloat16)
    grad = (
        lax.dot_general(
            context, error, (((0,), (0,)), ((), ())), preferred_element_type=jnp.float32
        )
        / rows
    )
    old = stale[0].astype(jnp.float32)
    flags = trigger[0].astype(jnp.float32)[:, None, None]
    blocked = (grad - old).reshape(blocks, span, width)
    squares = jnp.sum(blocked * blocked, axis=(1, 2))
    chosen = (blocked * flags).reshape(width, width)
    fresh = flags * grad.reshape(blocks, span, width) + (1.0 - flags) * old.reshape(
        blocks, span, width
    )
    stale_new = fresh.reshape(1, width, width).astype(jnp.bfloat16)
    norms = one_axis_at_a_time(squares, DP_SUB)
    count_dp = lax.axis_size(DP)
    count_sub = lax.axis_size(SUB)
    layered = chosen.reshape(count_dp, count_sub, owned, width)
    partial_sum = sent_and_summed(layered.astype(jnp.bfloat16), SUB, 1)
    summed = sent_and_summed(partial_sum.astype(jnp.bfloat16), DP, 0).reshape(owned, width)
    aggregate_new = aggregate + summed
    moment_new = 0.9 * moment + 0.1 * aggregate_new
    second_new = 0.999 * second + 0.001 * aggregate_new * aggregate_new
    weight_new = weight - 0.001 * (moment_new / (jnp.sqrt(second_new) + 1e-08) + 0.05 * weight)
    return (aggregate_new, weight_new, moment_new, second_new, stale_new, norms)


def solution(mesh):
    torus = Mesh(mesh.devices.reshape(4, 4, 2, 2, 4), ("dp_0", "dp_1", "dp_2", "sub_0", "sub_1"))
    placed = (
        P(DP_SUB, None),
        P(DP_SUB, None),
        P(DP_SUB, None),
        P(DP_SUB, None, None),
        P(DP_SUB, None),
        P(DP_SUB, None),
        P(DP_SUB, None),
        P(DP_SUB, None),
    )
    return jax.shard_map(
        body,
        mesh=torus,
        in_specs=placed,
        out_specs=(
            P(DP_SUB, None),
            P(DP_SUB, None),
            P(DP_SUB, None),
            P(DP_SUB, None),
            P(DP_SUB, None, None),
            P(),
        ),
        check_vma=False,
    )
```

profile of v0, /device:TPU:8, one launch (start us, length us, event | category | flops | bytes accessed | tf_op | source)
XLA Modules:
  0.0 231.7 jit_solution(8657969876965599879)
XLA Ops:
  7.2 0.0 copy-start
  7.2 0.0 all-gather.2.cloned.1.call-start
  7.2 0.9 convert_element_type.51
  8.1 20.3 %all_to_all.15 = bf16[8,4,1024]{2,1,0:T(4,128)(2,1)S(1)} all-to-all(bf16[8,4,1024]{2,1,0:T(4,128)(2,1)S(1)} %broadcast_in_dim.4), channel_id=1, replica_groups=mesh['dp_0'=4,'dp_1'=4,'dp_2'=2,'sub_0'=2,'sub_1'=4] {'sub_0','sub_1'}, dimensions={0} | all-to-all | bytes 131072 | tf_op jit(solution)/shard_map/all_to_all | solution.py:21
  28.4 0.6 reshape.67
  29.0 0.0 all-gather.2.cloned.1.call-update
  29.1 0.7 broadcast_multiply_fusion
  29.7 0.1 mul.107
  29.8 0.1 mul.108
  29.9 0.7 convert_bitcast_fusion
  30.5 0.1 mul.90
  30.6 0.1 mul.91
  30.7 0.1 mul.112
  30.8 0.1 mul.113
  30.8 54.6 %all-gather.2.cloned.1.call-done = bf16[1024,1024]{1,0:T(8,128)(2,1)} async-done(((bf16[32,1024]{1,0:T(8,128)(2,1)}), bf16[1024,1024]{1,0:T(8,128)(2,1)}) %all-gather.2.cloned.1.call-update) | async-done | bytes 2097168 | tf_op jit(solution)/shard_map/all_gather | solution.py:52
  85.5 0.0 copy-done
  85.5 14.1 %multiply_reduce_fusion = (f32[1024]{0:T(1024)S(1)}, f32[1024,1024]{1,0:T(8,128)}, bf16[1,1024,1024]{2,1,0:T(8,128)(2,1)}) fusion(bf16[1,1024,1024]{2,1,0:T(8,128)(2,1)} %param.11, f32[1024]{0:T(1024)S(1)} %mul.113, f32[1024]{0:T(1024)S(1)} %mul.108, bf16[1576,1024]{1,0:T(8,128)(2,1)S(1)} %copy-done, bf16[1576,1024]{1,0:T(8,128)(2,1)} %param.9, ...), kind=kOutput, calls=%fused_computation.7 | convolution fusion | flops 6624500736 | bytes 16953344 | tf_op jit(solution)/shard_map/dot_general | solution.py:56
  99.6 5.2 %reshape.68 = f32[32,8,1,4,1024]{4,3,1,0,2:T(4,128)} reshape(f32[1024,1024]{1,0:T(8,128)} %get-tuple-element.7) | data formatting | bytes 8388608 | tf_op jit(solution)/shard_map/reshape | solution.py:63
  104.7 4.7 %fusion.3 = bf16[8,32,1,4,1024]{4,0,3,2,1:T(8,128)(2,1)S(1)} fusion(f32[32,8,1,4,1024]{4,3,1,0,2:T(4,128)} %reshape.68, f32[32]{0:T(128)S(1)} %mul.91), kind=kLoop, calls=%fused_computation.8 | loop fusion | flops 2097152 | bytes 6291584 | tf_op jit(solution)/shard_map/transpose | solution.py:35
  109.4 1.6 copy.18
  111.1 0.0 copy-start.1
  111.1 0.0 copy-start.2
  111.1 0.0 copy-start.3
  111.1 58.8 %all_to_all.16 = bf16[8,32,1,4,1024]{4,3,1,2,0:T(4,128)(2,1)} all-to-all(bf16[8,32,1,4,1024]{4,3,1,2,0:T(4,128)(2,1)S(1)} %copy.18), channel_id=1, replica_groups=mesh['dp_0'=4,'dp_1'=4,'dp_2'=2,'sub_0'=2,'sub_1'=4] {'sub_0','sub_1'}, dimensions={0} | all-to-all | bytes 4194304 | tf_op jit(solution)/shard_map/all_to_all | solution.py:40
  169.9 3.3 %reduce_sum.37 = bf16[32,4,1024]{2,1,0:T(4,128)(2,1)} reduce(bf16[8,32,1,4,1024]{4,3,1,2,0:T(4,128)(2,1)} %all_to_all.16, bf16[]{:T(256)} %constant.3.clone.1), dimensions={0,2}, to_apply=%region_0.0 | reduce | flops 917504 | bytes 2359298 | tf_op jit(solution)/shard_map/reduce_sum | solution.py:41
  173.3 6.1 %all-to-all-start.2 = ((bf16[32,1,1,4,1024]{4,3,2,1,0:T(4,128)(2,1)}), bf16[32,1,1,4,1024]{4,3,2,1,0:T(4,128)(2,1)S(1)}, u32[]{:S(2)}, u32[]{:S(2)}) async-start(bf16[32,1,1,4,1024]{4,3,2,1,0:T(4,128)(2,1)} %bitcast.4), calls=%async_computation.2 | async-start | bytes 524288 | tf_op jit(solution)/shard_map/all_to_all | solution.py:40
  179.4 0.1 reduce_sum.40
  179.5 0.1 reduce_sum.41
  179.6 10.8 %psum.35 = f32[16]{0:T(128)S(1)} all-reduce(f32[16]{0:T(128)S(1)} %reduce_sum.41), channel_id=1, replica_groups=mesh['dp_0'=4,'dp_1'=4,'dp_2'=2,'sub_0'=2,'sub_1'=4] {'dp_0'}, use_global_device_ids=true, to_apply=%region_4.0 | all-reduce | flops 16 | bytes 128 | tf_op jit(solution)/shard_map/psum | solution.py:29
  190.4 11.6 %psum.36 = f32[16]{0:T(128)S(1)} all-reduce(f32[16]{0:T(128)S(1)} %psum.35), channel_id=1, replica_groups=mesh['dp_0'=4,'dp_1'=4,'dp_2'=2,'sub_0'=2,'sub_1'=4] {'dp_1'}, use_global_device_ids=true, to_apply=%region_5.0 | all-reduce | flops 16 | bytes 128 | tf_op jit(solution)/shard_map/psum | solution.py:29
  202.0 2.5 %psum.37 = f32[16]{0:T(128)S(1)} all-reduce(f32[16]{0:T(128)S(1)} %psum.36), channel_id=1, replica_groups=mesh['dp_0'=4,'dp_1'=4,'dp_2'=2,'sub_0'=2,'sub_1'=4] {'dp_2'}, use_global_device_ids=true, to_apply=%region_6.0 | all-reduce | flops 16 | bytes 128 | tf_op jit(solution)/shard_map/psum | solution.py:29
  204.5 8.8 %psum.38 = f32[16]{0:T(128)S(1)} all-reduce(f32[16]{0:T(128)S(1)} %psum.37), channel_id=1, replica_groups=mesh['dp_0'=4,'dp_1'=4,'dp_2'=2,'sub_0'=2,'sub_1'=4] {'sub_0'}, use_global_device_ids=true, to_apply=%region_7.0 | all-reduce | flops 16 | bytes 128 | tf_op jit(solution)/shard_map/psum | solution.py:29
  213.3 10.0 %psum.39 = f32[16]{0:T(128)} all-reduce(f32[16]{0:T(128)S(1)} %psum.38), channel_id=1, replica_groups=mesh['dp_0'=4,'dp_1'=4,'dp_2'=2,'sub_0'=2,'sub_1'=4] {'sub_1'}, use_global_device_ids=true, to_apply=%region_8.9 | all-reduce | flops 16 | bytes 128 | tf_op jit(solution)/shard_map/psum | solution.py:29
  223.3 0.0 all-to-all-done.2
  223.3 0.1 convert_reduce_fusion
  223.4 0.0 copy-done.1
  223.4 0.0 copy-done.2
  223.4 0.0 copy-done.3
  223.4 1.4 multiply_subtract_fusion
  (1 shorter events, 0.0 us)
Async XLA Ops:
  7.2 78.3 %copy-start = (bf16[1576,1024]{1,0:T(8,128)(2,1)S(1)}, bf16[1576,1024]{1,0:T(8,128)(2,1)}, u32[]{:S(2)}) copy-start(bf16[1576,1024]{1,0:T(8,128)(2,1)} %param.8) | copy-start | bytes 9682948
  7.2 78.3 %all-gather.2.cloned.1.call-start = ((), (), s32[]{:S(2)}) async-start(), calls=%async_computation.3 | async-start | bytes 2162688 | tf_op jit(solution)/shard_map/all_gather | solution.py:52
  111.1 112.4 %copy-start.1 = (f32[4,1024]{1,0:T(4,128)S(1)}, f32[4,1024]{1,0:T(4,128)}, u32[]{:S(2)}) copy-start(f32[4,1024]{1,0:T(4,128)} %param.10) | copy-start | bytes 49156
  111.1 112.4 %copy-start.2 = (f32[4,1024]{1,0:T(4,128)S(1)}, f32[4,1024]{1,0:T(4,128)}, u32[]{:S(2)}) copy-start(f32[4,1024]{1,0:T(4,128)} %param.15) | copy-start | bytes 49156
  111.1 112.4 %copy-start.3 = (f32[4,1024]{1,0:T(4,128)S(1)}, f32[4,1024]{1,0:T(4,128)}, u32[]{:S(2)}) copy-start(f32[4,1024]{1,0:T(4,128)} %param.14) | copy-start | bytes 49156
  173.3 50.0 %all-to-all-start.2 = ((bf16[32,1,1,4,1024]{4,3,2,1,0:T(4,128)(2,1)}), bf16[32,1,1,4,1024]{4,3,2,1,0:T(4,128)(2,1)S(1)}, u32[]{:S(2)}, u32[]{:S(2)}) async-start(bf16[32,1,1,4,1024]{4,3,2,1,0:T(4,128)(2,1)} %bitcast.4), calls=%async_computation.2 | async-start | bytes 524288 | tf_op jit(solution)/shard_map/all_to_all | solution.py:40
Sparse Core Ops, SparseCore 0:
  29.2 56.2 all-gather.1
where the time goes:
time: 232 us
  blocking collectives  123 us (53%)
  waiting for transfers between devices  54.6 us (24%)
  matrix products  14.1 us (6%)
  between operations  14.1 us (6%)
  other arithmetic  11.8 us (5%)
  local copies, waits for them, and re-layouts  8 us (3%)
  starting transfers between devices  6.18 us (3%)
    all_to_all x1, blocking collectives, sent_and_summed(): lax.all_to_all(pieces, axis, split_axis=0, concat_axis=0, tiled=True)  58.8 us
    all_gather x1, waiting for transfers between devices, body(): low_whole = lax.all_gather(low_group, DP, axis=0, tiled=True)  54.6 us
    psum x5, blocking collectives, one_axis_at_a_time(): return functools.reduce(lax.psum, axes, value)  43.7 us
    all_to_all x1, blocking collectives, sent_to_all(): return lax.all_to_all(copies, axis, split_axis=0, concat_axis=0, tiled=True)  20.3 us
    dot_general x1, matrix products, body(): lax.dot_general(context, error, (((0,), (0,)), ((), ())), preferred_eleme...  14.1 us
    all_to_all x1, starting transfers between devices, sent_and_summed(): lax.all_to_all(pieces, axis, split_axis=0, concat_axis=0, tiled=True)  6.14 us
    reshape x1, local copies, waits for them, and re-layouts, body(): blocked = (grad - old).reshape(blocks, span, width)  5.17 us
    transpose x1, other arithmetic, in_blocks(): return jnp.moveaxis(pieces, dim, 0)  4.68 us
  transfers between devices with their start and end apart: 2, of which 1 were waited for; matrix products, arithmetic and copies ran while one was open for 1% of the time, Pallas kernels for 0%

commit v1 on v0

--- a/solution.py
+++ b/solution.py
@@ -49,7 +49,9 @@
     span = width // blocks
     low_rows = weight.astype(jnp.bfloat16)
     low_group = gathered_copies(low_rows, SUB, 0)
-    low_whole = lax.all_gather(low_group, DP, axis=0, tiled=True)
+    low_whole = jnp.concatenate(
+        lax.all_to_all(jnp.stack([low_group] * lax.axis_size(DP)), DP, 0, 0), axis=0
+    )
     output = jnp.dot(context, low_whole, preferred_element_type=jnp.float32)
     error = (output - target.astype(jnp.float32)).astype(jnp.bfloat16)
     grad = (

time: 232 us -> 213 us (0.918)
  between operations: 14.1 us -> 0.74 us
  blocking collectives: 123 us -> 117 us
  starting transfers between devices: 6.18 us -> 10.9 us
  waiting for transfers between devices: 54.6 us -> 49.9 us
    all_gather x1 -> x0, waiting for transfers between devices: 54.6 us -> none  [body(): low_whole = lax.all_gather(low_group, DP, axis=0, tiled=True)]
    all_to_all x0 -> x1, waiting for transfers between devices: none -> 49.9 us  [body(): lax.all_to_all(jnp.stack([low_group] * lax.axis_size(DP)), DP, 0, 0)]
    all_to_all x0 -> x1, starting transfers between devices: none -> 6.18 us  [body(): lax.all_to_all(jnp.stack([low_group] * lax.axis_size(DP)), DP, 0, 0)]
    all_to_all x1, blocking collectives: 58.8 us -> 53.1 us  [sent_and_summed(): lax.all_to_all(pieces, axis, split_axis=0, concat_axis=0, tiled=True)]
  transfers between devices with their start and end apart: 2 -> 2, of which waited for: 1 -> 1; matrix products, arithmetic and copies ran while one was open for 1% -> 0% of each run, Pallas kernels for 0% -> 0%
where the time goes in v1:
time: 213 us; the launch traced here: 212 us
  blocking collectives  117 us (55%)
  waiting for transfers between devices  49.9 us (23%)
  matrix products  14.1 us (7%)
  starting transfers between devices  10.9 us (5%)
  other arithmetic  10.5 us (5%)
  local copies, waits for them, and re-layouts  8.96 us (4%)
    all_to_all x1, blocking collectives, sent_and_summed(): lax.all_to_all(pieces, axis, split_axis=0, concat_axis=0, tiled=True)  53.1 us
    all_to_all x1, waiting for transfers between devices, body(): lax.all_to_all(jnp.stack([low_group] * lax.axis_size(DP)), DP, 0, 0)  49.9 us
    psum x5, blocking collectives, one_axis_at_a_time(): return functools.reduce(lax.psum, axes, value)  43.8 us
    all_to_all x1, blocking collectives, sent_to_all(): return lax.all_to_all(copies, axis, split_axis=0, concat_axis=0, tiled=True)  20.3 us
    dot_general x1, matrix products, body(): lax.dot_general(context, error, (((0,), (0,)), ((), ())), preferred_eleme...  14.1 us
    all_to_all x1, starting transfers between devices, body(): lax.all_to_all(jnp.stack([low_group] * lax.axis_size(DP)), DP, 0, 0)  6.18 us
    reshape x1, local copies, waits for them, and re-layouts, body(): blocked = (grad - old).reshape(blocks, span, width)  5.17 us
    transpose x1, other arithmetic, in_blocks(): return jnp.moveaxis(pieces, dim, 0)  4.68 us
  transfers between devices with their start and end apart: 2, of which 1 were waited for; matrix products, arithmetic and copies ran while one was open for 0% of the time, Pallas kernels for 0%

profile of v1, /device:TPU:8, one launch (start us, length us, event | category | flops | bytes accessed | tf_op | source)
XLA Modules:
  0.0 212.2 jit_solution(15444562218909207861)
XLA Ops:
  0.6 0.0 copy-start
  0.6 0.9 convert_element_type.51
  1.5 20.3 %all_to_all.20 = bf16[8,4,1024]{2,1,0:T(4,128)(2,1)S(1)} all-to-all(bf16[8,4,1024]{2,1,0:T(4,128)(2,1)S(1)} %broadcast_in_dim.4), channel_id=1, replica_groups=mesh['dp_0'=4,'dp_1'=4,'dp_2'=2,'sub_0'=2,'sub_1'=4] {'sub_0','sub_1'}, dimensions={0} | all-to-all | bytes 131072 | tf_op jit(solution)/shard_map/all_to_all | solution.py:21
  21.8 0.0 copy-start.4
  21.8 1.6 stack.3
  23.4 6.2 %all-to-all-start.1 = ((bf16[32,32,1024]{2,1,0:T(8,128)(2,1)}), bf16[32,32,1024]{2,1,0:T(8,128)(2,1)}, u32[]{:S(2)}, u32[]{:S(2)}) async-start(bf16[32,32,1024]{2,1,0:T(8,128)(2,1)} %stack.3), calls=%async_computation.1 | async-start | bytes 4194304 | tf_op jit(solution)/shard_map/all_to_all | solution.py:53
  29.6 0.0 copy-done.4
  29.6 0.1 mul.107
  29.7 0.1 mul.108
  29.8 0.1 mul.90
  29.9 0.1 mul.91
  29.9 0.1 mul.112
  30.0 0.1 mul.113
  30.1 49.9 %all-to-all-done.1 = bf16[32,32,1024]{2,1,0:T(8,128)(2,1)} async-done(((bf16[32,32,1024]{2,1,0:T(8,128)(2,1)}), bf16[32,32,1024]{2,1,0:T(8,128)(2,1)}, u32[]{:S(2)}, u32[]{:S(2)}) %all-to-all-start.1) | async-done | bytes 2097184 | tf_op jit(solution)/shard_map/all_to_all | solution.py:53
  80.0 0.0 copy-done
  80.0 14.1 %multiply_reduce_fusion = (f32[1024]{0:T(1024)S(1)}, f32[1024,1024]{1,0:T(8,128)}, bf16[1,1024,1024]{2,1,0:T(8,128)(2,1)}) fusion(bf16[1,1024,1024]{2,1,0:T(8,128)(2,1)} %param.11, f32[1024]{0:T(1024)S(1)} %mul.113, f32[1024]{0:T(1024)S(1)} %mul.108, bf16[1576,1024]{1,0:T(8,128)(2,1)S(1)} %copy-done, bf16[1576,1024]{1,0:T(8,128)(2,1)} %param.9, ...), kind=kOutput, calls=%fused_computation.7 | convolution fusion | flops 6624500736 | bytes 16953344 | tf_op jit(solution)/shard_map/dot_general | solution.py:58
  94.1 5.2 %reshape.70 = f32[32,8,1,4,1024]{4,3,1,0,2:T(4,128)} reshape(f32[1024,1024]{1,0:T(8,128)} %get-tuple-element.7) | data formatting | bytes 8388608 | tf_op jit(solution)/shard_map/reshape | solution.py:65
  99.3 4.7 %fusion.3 = bf16[8,32,1,4,1024]{4,0,3,2,1:T(8,128)(2,1)S(1)} fusion(f32[32,8,1,4,1024]{4,3,1,0,2:T(4,128)} %reshape.70, f32[32]{0:T(128)S(1)} %mul.91), kind=kLoop, calls=%fused_computation.8 | loop fusion | flops 2097152 | bytes 6291584 | tf_op jit(solution)/shard_map/transpose | solution.py:35
  104.0 1.6 copy.18
  105.6 0.0 copy-start.1
  105.6 0.0 copy-start.2
  105.6 0.0 copy-start.3
  105.6 53.1 %all_to_all.21 = bf16[8,32,1,4,1024]{4,3,1,2,0:T(4,128)(2,1)} all-to-all(bf16[8,32,1,4,1024]{4,3,1,2,0:T(4,128)(2,1)S(1)} %copy.18), channel_id=1, replica_groups=mesh['dp_0'=4,'dp_1'=4,'dp_2'=2,'sub_0'=2,'sub_1'=4] {'sub_0','sub_1'}, dimensions={0} | all-to-all | bytes 4194304 | tf_op jit(solution)/shard_map/all_to_all | solution.py:40
  158.7 3.3 %reduce_sum.37 = bf16[32,4,1024]{2,1,0:T(4,128)(2,1)} reduce(bf16[8,32,1,4,1024]{4,3,1,2,0:T(4,128)(2,1)} %all_to_all.21, bf16[]{:T(256)} %constant.3.clone.1), dimensions={0,2}, to_apply=%region_0.0 | reduce | flops 917504 | bytes 2359298 | tf_op jit(solution)/shard_map/reduce_sum | solution.py:41
  162.1 4.7 %all-to-all-start.3 = ((bf16[32,1,1,4,1024]{4,3,2,1,0:T(4,128)(2,1)}), bf16[32,1,1,4,1024]{4,3,2,1,0:T(4,128)(2,1)S(1)}, u32[]{:S(2)}, u32[]{:S(2)}) async-start(bf16[32,1,1,4,1024]{4,3,2,1,0:T(4,128)(2,1)} %bitcast.5), calls=%async_computation.3 | async-start | bytes 524288 | tf_op jit(solution)/shard_map/all_to_all | solution.py:40
  166.7 0.1 reduce_sum.40
  166.8 0.1 reduce_sum.41
  166.9 10.8 %psum.35 = f32[16]{0:T(128)S(1)} all-reduce(f32[16]{0:T(128)S(1)} %reduce_sum.41), channel_id=1, replica_groups=mesh['dp_0'=4,'dp_1'=4,'dp_2'=2,'sub_0'=2,'sub_1'=4] {'dp_0'}, use_global_device_ids=true, to_apply=%region_4.0 | all-reduce | flops 16 | bytes 128 | tf_op jit(solution)/shard_map/psum | solution.py:29
  177.7 11.6 %psum.36 = f32[16]{0:T(128)S(1)} all-reduce(f32[16]{0:T(128)S(1)} %psum.35), channel_id=1, replica_groups=mesh['dp_0'=4,'dp_1'=4,'dp_2'=2,'sub_0'=2,'sub_1'=4] {'dp_1'}, use_global_device_ids=true, to_apply=%region_5.0 | all-reduce | flops 16 | bytes 128 | tf_op jit(solution)/shard_map/psum | solution.py:29
  189.3 2.5 %psum.37 = f32[16]{0:T(128)S(1)} all-reduce(f32[16]{0:T(128)S(1)} %psum.36), channel_id=1, replica_groups=mesh['dp_0'=4,'dp_1'=4,'dp_2'=2,'sub_0'=2,'sub_1'=4] {'dp_2'}, use_global_device_ids=true, to_apply=%region_6.0 | all-reduce | flops 16 | bytes 128 | tf_op jit(solution)/shard_map/psum | solution.py:29
  191.8 8.8 %psum.38 = f32[16]{0:T(128)S(1)} all-reduce(f32[16]{0:T(128)S(1)} %psum.37), channel_id=1, replica_groups=mesh['dp_0'=4,'dp_1'=4,'dp_2'=2,'sub_0'=2,'sub_1'=4] {'sub_0'}, use_global_device_ids=true, to_apply=%region_7.0 | all-reduce | flops 16 | bytes 128 | tf_op jit(solution)/shard_map/psum | solution.py:29
  200.6 10.1 %psum.39 = f32[16]{0:T(128)} all-reduce(f32[16]{0:T(128)S(1)} %psum.38), channel_id=1, replica_groups=mesh['dp_0'=4,'dp_1'=4,'dp_2'=2,'sub_0'=2,'sub_1'=4] {'sub_1'}, use_global_device_ids=true, to_apply=%region_8.9 | all-reduce | flops 16 | bytes 128 | tf_op jit(solution)/shard_map/psum | solution.py:29
  210.7 0.0 all-to-all-done.3
  210.7 0.1 convert_reduce_fusion
  210.9 0.0 copy-done.1
  210.9 0.0 copy-done.2
  210.9 0.0 copy-done.3
  210.9 1.4 multiply_subtract_fusion
  (4 shorter events, 0.0 us)
Async XLA Ops:
  0.6 79.4 %copy-start = (bf16[1576,1024]{1,0:T(8,128)(2,1)S(1)}, bf16[1576,1024]{1,0:T(8,128)(2,1)}, u32[]{:S(2)}) copy-start(bf16[1576,1024]{1,0:T(8,128)(2,1)} %param.8) | copy-start | bytes 9682948
  21.8 7.8 %copy-start.4 = (s32[1,16]{1,0:T(1,128)S(1)}, s32[1,16]{1,0:T(1,128)}, u32[]{:S(2)}) copy-start(s32[1,16]{1,0:T(1,128)} %param.12) | copy-start | bytes 196
  23.4 56.6 %all-to-all-start.1 = ((bf16[32,32,1024]{2,1,0:T(8,128)(2,1)}), bf16[32,32,1024]{2,1,0:T(8,128)(2,1)}, u32[]{:S(2)}, u32[]{:S(2)}) async-start(bf16[32,32,1024]{2,1,0:T(8,128)(2,1)} %stack.3), calls=%async_computation.1 | async-start | bytes 4194304 | tf_op jit(solution)/shard_map/all_to_all | solution.py:53
  105.6 105.3 %copy-start.1 = (f32[4,1024]{1,0:T(4,128)S(1)}, f32[4,1024]{1,0:T(4,128)}, u32[]{:S(2)}) copy-start(f32[4,1024]{1,0:T(4,128)} %param.10) | copy-start | bytes 49156
  105.6 105.2 %copy-start.2 = (f32[4,1024]{1,0:T(4,128)S(1)}, f32[4,1024]{1,0:T(4,128)}, u32[]{:S(2)}) copy-start(f32[4,1024]{1,0:T(4,128)} %param.15) | copy-start | bytes 49156
  105.6 105.2 %copy-start.3 = (f32[4,1024]{1,0:T(4,128)S(1)}, f32[4,1024]{1,0:T(4,128)}, u32[]{:S(2)}) copy-start(f32[4,1024]{1,0:T(4,128)} %param.14) | copy-start | bytes 49156
  162.1 48.7 %all-to-all-start.3 = ((bf16[32,1,1,4,1024]{4,3,2,1,0:T(4,128)(2,1)}), bf16[32,1,1,4,1024]{4,3,2,1,0:T(4,128)(2,1)S(1)}, u32[]{:S(2)}, u32[]{:S(2)}) async-start(bf16[32,1,1,4,1024]{4,3,2,1,0:T(4,128)(2,1)} %bitcast.5), calls=%async_computation.3 | async-start | bytes 524288 | tf_op jit(solution)/shard_map/all_to_all | solution.py:40
